TPU v7x, 32 devices: a whole 2x2x4 slice. The times are simulated.
32 devices in a mesh: groups: 2 (over y), seq: 4 (over z), exp: 2 (over x), rep: 2 (over core).
Axes of the slice: x: 2, y: 2, z: 4, core: 2. Of those that a mesh axis runs over, the one named last changes fastest.
Arguments:
- queries: bfloat16 [512, 4096], P(('groups', 'seq'), ('exp', 'rep')), parts along dimension 0, may hold values from -4 to 4
- key_rows: bfloat16 [512, 4096], P(('groups', 'seq'), ('exp', 'rep')), parts along dimension 0, may hold values from -4 to 4
- value_rows: bfloat16 [512, 4096], P(('groups', 'seq'), ('exp', 'rep')), parts along dimension 0, may hold values from -6 to 6
- decay_log: float32 [512, 32], P(('groups', 'seq'), ('exp', 'rep')), parts along dimension 0, may hold values from -1.5 to 0
- residual: bfloat16 [512, 4096], P(('groups', 'seq'), ('exp', 'rep')), parts along dimension 0, may hold values from -6 to 6
- out_gate: bfloat16 [512, 4096], P(('groups', 'seq'), ('exp', 'rep')), parts along dimension 0, may hold values from -6 to 6
- attn_gain: float32 [4096], P(('exp', 'rep')), may hold values from 0.1 to 1.9
- moe_gain: float32 [4096], P(('exp', 'rep')), may hold values from 0.1 to 1.9
- routes: int32 [512, 2], P(('groups', 'seq')), parts along dimension 0, may hold values from 0 to 31, as said below
- route_weights: float32 [512, 2], P(('groups', 'seq')), parts along dimension 0, may hold values from 0.3 to 1
- w_gate: bfloat16 [2, 4608, 4096], P('exp', 'seq'), may hold values from -0.09375 to 0.09375
- w_up: bfloat16 [2, 4608, 4096], P('exp', 'seq'), may hold values from -0.09375 to 0.09375
- w_down: bfloat16 [2, 4608, 4096], P('exp', 'seq'), may hold values from -0.09375 to 0.09375
Outputs:
- layer_out: bfloat16 [512, 4096], P(('groups', 'seq'), ('exp', 'rep')), parts along dimension 0
There are 2 independent parts, one for each index of `groups`. A program takes and returns all parts, laid end to end along the dimension named above; an argument that names none is the same for every part. Nothing has to cross between parts.
Inputs may be any that keep to these rules, and one draw needn't show every extreme that they name: `routes`: each row names two different experts. Within each aligned block of 64 rows no expert is named by more than 6 rows, every expert is named in every block, and one expert below 2 is named by exactly 6 rows in every block.
All inputs are finite; a program needn't handle non-finite values.
Results may differ from a plain program's by a relative error of at most 0.01.
Values may be sent and summed in bfloat16 or wider, within the bound.
A program may use at most 64 MiB of HBM per device.

v0:
```python
import jax
import jax.numpy as jnp
from jax import lax
from jax.sharding import PartitionSpec as P

CAP = 6


EPSILON = 1e-06


def from_behind(block, axis, distance):
    devices = range(lax.axis_size(axis))
    route = [(i - distance, i) for i in devices if i - distance in devices]
    return lax.ppermute(block, axis, route)


def slot_tables(route_block, weight_block, experts, capacity):
    expert_ids = jnp.arange(experts, dtype=jnp.int32)
    onehot = (route_block[:, :, None] == expert_ids[None, None, :]).astype(jnp.int32)
    tokens = route_block.shape[0]
    flat_hits = onehot.reshape(tokens * 2, experts)
    before = jnp.cumsum(flat_hits, axis=0) - flat_hits
    places = jnp.arange(capacity, dtype=jnp.int32)
    hit_table = flat_hits[:, :, None] * (before[:, :, None] == places[None, None, :]).astype(
        jnp.int32
    )
    hit_table = hit_table.astype(jnp.float32).reshape(tokens, 2, experts * capacity)
    dispatch = jnp.sum(hit_table, axis=1)
    combine = jnp.sum(hit_table * weight_block[:, :, None], axis=1)
    return (dispatch, combine)


def project_rows(slot_rows, weight_rows):
    return lax.dot_general(
        slot_rows, weight_rows, (((1,), (1,)), ((), ())), preferred_element_type=jnp.float32
    )


def shards(
    queries,
    key_rows,
    value_rows,
    decay_log,
    residual,
    out_gate,
    attn_gain,
    moe_gain,
    routes,
    route_weights,
    w_gate,
    w_up,
    w_down,
):
    tokens, columns = queries.shape
    heads_dev = decay_log.shape[1]
    head_dim = columns // heads_dev
    query_heads = queries.reshape(tokens, heads_dev, head_dim)
    key_heads = key_rows.reshape(tokens, heads_dev, head_dim)
    value_heads = value_rows.reshape(tokens, heads_dev, head_dim)
    cumulative = jnp.cumsum(decay_log, axis=0)
    token_positions = jnp.arange(tokens)
    causal = (token_positions[:, None] >= token_positions[None, :])[:, :, None]
    log_gaps = cumulative[:, None, :] - cumulative[None, :, :]
    decay_mask = jnp.where(causal, jnp.exp(jnp.where(causal, log_gaps, 0.0)), 0.0)
    scores = jnp.einsum("thd,jhd->htj", query_heads, key_heads, preferred_element_type=jnp.float32)
    mixing = (scores * jnp.transpose(decay_mask, (2, 0, 1))).astype(jnp.bfloat16)
    local_part = jnp.einsum("htj,jhd->thd", mixing, value_heads, preferred_element_type=jnp.float32)
    ending = cumulative[-1]
    faded_keys = key_heads.astype(jnp.float32) * jnp.exp(ending[None, :] - cumulative)[:, :, None]
    block_state = jnp.einsum(
        "jhd,jhe->hde", faded_keys, value_heads.astype(jnp.float32), precision=lax.Precision.HIGHEST
    )
    fading = jnp.exp(ending)
    zeros_state = jnp.zeros_like(block_state)

    def advance(index_step, carried):
        return from_behind(
            (fading[:, None, None] * carried + block_state).astype(jnp.bfloat16), "seq", 1
        ).astype(jnp.float32)

    incoming = lax.fori_loop(0, lax.axis_size("seq") - 1, advance, zeros_state)
    lifted = query_heads.astype(jnp.float32) * jnp.exp(cumulative)[:, :, None]
    carried_part = jnp.einsum("thd,hde->the", lifted, incoming, precision=lax.Precision.HIGHEST)
    attended = (local_part + carried_part).reshape(tokens, columns)
    column_groups = lax.axis_size(("exp", "rep"))
    full_width = columns * column_groups
    attn_sumsq = lax.psum(jnp.sum(attended * attended, axis=1), ("exp", "rep"))
    attn_scale = lax.rsqrt(attn_sumsq[:, None] / full_width + EPSILON)
    hidden = residual.astype(jnp.float32) + jax.nn.sigmoid(out_gate.astype(jnp.float32)) * (
        attended * attn_scale * attn_gain
    )
    moe_sumsq = lax.psum(jnp.sum(hidden * hidden, axis=1), ("exp", "rep"))
    normed = (hidden * lax.rsqrt(moe_sumsq[:, None] / full_width + EPSILON) * moe_gain).astype(
        jnp.bfloat16
    )
    experts = lax.axis_size("exp")
    copies = lax.axis_size("rep")
    half_cap = CAP // copies
    dispatch, combine = slot_tables(routes, route_weights, experts, CAP)
    packed = jnp.dot(
        jnp.transpose(dispatch).astype(jnp.bfloat16), normed, preferred_element_type=jnp.float32
    ).astype(jnp.bfloat16)
    packed = packed.reshape(experts * copies, half_cap, columns)
    arrived = lax.all_to_all(packed, ("exp", "rep"), split_axis=0, concat_axis=2, tiled=True)
    rows_local = arrived.reshape(half_cap, full_width)
    gate_mat = w_gate[0]
    up_mat = w_up[0]
    down_mat = w_down[0]
    gathered = lax.all_gather(rows_local, "seq", axis=0, tiled=True)
    gate_val = project_rows(gathered, gate_mat)
    up_val = project_rows(gathered, up_mat)
    summed = lax.psum_scatter(
        jnp.dot(
            (jax.nn.silu(gate_val) * up_val).astype(jnp.bfloat16),
            down_mat,
            preferred_element_type=jnp.float32,
        ).astype(jnp.bfloat16),
        "seq",
        scatter_dimension=0,
        tiled=True,
    )
    coming_back = lax.all_to_all(
        summed.reshape(half_cap, column_groups, columns),
        ("exp", "rep"),
        split_axis=1,
        concat_axis=0,
        tiled=True,
    )
    coming_back = coming_back.reshape(experts * CAP, columns)
    expert_mix = jnp.dot(combine, coming_back.astype(jnp.float32), precision=lax.Precision.HIGHEST)
    return (hidden + expert_mix).astype(jnp.bfloat16)


def solution(mesh):
    return jax.shard_map(
        shards,
        mesh=mesh,
        in_specs=(
            P(("groups", "seq"), ("exp", "rep")),
            P(("groups", "seq"), ("exp", "rep")),
            P(("groups", "seq"), ("exp", "rep")),
            P(("groups", "seq"), ("exp", "rep")),
            P(("groups", "seq"), ("exp", "rep")),
            P(("groups", "seq"), ("exp", "rep")),
            P(("exp", "rep")),
            P(("exp", "rep")),
            P(("groups", "seq"), None),
            P(("groups", "seq"), None),
            P("exp", "seq", None),
            P("exp", "seq", None),
            P("exp", "seq", None),
        ),
        out_specs=P(("groups", "seq"), ("exp", "rep")),
        check_vma=False,
    )
```

profile of v0, /device:TPU:0, one launch (start us, length us, event | category | flops | bytes accessed | tf_op | source)
XLA Modules:
  0.0 143.3 jit_solution(10298115426524327892)
XLA Ops:
  6.6 0.9 copy.34
  7.9 1.6 %fusion.27 = f32[8,128,128]{2,1,0:T(8,128)S(1)} fusion(f32[64,8]{0,1:T(8,128)S(1)} %copy.39, bf16[64,1024]{1,0:T(8,128)(2,1)S(1)} %copy-done, bf16[64,1024]{1,0:T(8,128)(2,1)} %param.16), kind=kOutput, calls=%fused_computation.29 | convolution fusion | flops 100794368 | bytes 788480 | tf_op jit(solution)/shard_map/jhd,jhe->hde/dot_general | solution.py:71
  9.5 1.3 convolution_bitcast_fusion.1
  10.8 28.4 %while.11 = (s32[]{:T(128)}, f32[8,128,128]{2,1,0:T(8,128)S(1)}, f32[8]{0:T(128)S(1)}, f32[8,128,128]{2,1,0:T(8,128)S(1)}, s32[]{:T(128)}, /*index=5*/s32[]{:T(128)}) while((s32[]{:T(128)}, f32[8,128,128]{2,1,0:T(8,128)S(1)}, f32[8]{0:T(128)S(1)}, f32[8,128,128]{2,1,0:T(8,128)S(1)}, s32[]{:T(128)}, /*index=5*/s32[]{:T(128)}) %tuple.26), condition=%wide.region_2.3_spmd.clone, body=%wide.region_1.2_spmd.clone.sunk | while | flops 655363 | bytes 3145879 | solution.py:82
  10.9 5.0 %collective-permute-start = (bf16[8,128,128]{2,1,0:T(8,128)(2,1)S(1)}, bf16[8,128,128]{2,1,0:T(8,128)(2,1)S(1)}, u32[]{:S(2)}, u32[]{:S(2)}) collective-permute-start(bf16[8,128,128]{2,1,0:T(8,128)(2,1)S(1)} %fusion.88), channel_id=1, source_target_pairs={{0,4},{4,8},{8,12},{1,5},{5,9},{9,13},{2,6},{6,10},{10,14},{3,7},{... | collective-permute-start | bytes 786440 | tf_op jit(solution)/shard_map/while/body/eval_jaxpr/ppermute | solution.py:15
  15.9 5.5 %collective-permute-done = bf16[8,128,128]{2,1,0:T(8,128)(2,1)S(1)} collective-permute-done((bf16[8,128,128]{2,1,0:T(8,128)(2,1)S(1)}, bf16[8,128,128]{2,1,0:T(8,128)(2,1)S(1)}, u32[]{:S(2)}, u32[]{:S(2)}) %collective-permute-start) | collective-permute-done | bytes 262176 | tf_op jit(solution)/shard_map/while/body/eval_jaxpr/ppermute | solution.py:15
  21.5 0.1 fusion.88
  21.6 4.4 %collective-permute-start = (bf16[8,128,128]{2,1,0:T(8,128)(2,1)S(1)}, bf16[8,128,128]{2,1,0:T(8,128)(2,1)S(1)}, u32[]{:S(2)}, u32[]{:S(2)}) collective-permute-start(bf16[8,128,128]{2,1,0:T(8,128)(2,1)S(1)} %fusion.88), channel_id=1, source_target_pairs={{0,4},{4,8},{8,12},{1,5},{5,9},{9,13},{2,6},{6,10},{10,14},{3,7},{... | collective-permute-start | bytes 786440 | tf_op jit(solution)/shard_map/while/body/eval_jaxpr/ppermute | solution.py:15
  26.0 4.7 %collective-permute-done = bf16[8,128,128]{2,1,0:T(8,128)(2,1)S(1)} collective-permute-done((bf16[8,128,128]{2,1,0:T(8,128)(2,1)S(1)}, bf16[8,128,128]{2,1,0:T(8,128)(2,1)S(1)}, u32[]{:S(2)}, u32[]{:S(2)}) %collective-permute-start) | collective-permute-done | bytes 262176 | tf_op jit(solution)/shard_map/while/body/eval_jaxpr/ppermute | solution.py:15
  30.9 4.4 %collective-permute-start = (bf16[8,128,128]{2,1,0:T(8,128)(2,1)S(1)}, bf16[8,128,128]{2,1,0:T(8,128)(2,1)S(1)}, u32[]{:S(2)}, u32[]{:S(2)}) collective-permute-start(bf16[8,128,128]{2,1,0:T(8,128)(2,1)S(1)} %fusion.88), channel_id=1, source_target_pairs={{0,4},{4,8},{8,12},{1,5},{5,9},{9,13},{2,6},{6,10},{10,14},{3,7},{... | collective-permute-start | bytes 786440 | tf_op jit(solution)/shard_map/while/body/eval_jaxpr/ppermute | solution.py:15
  35.3 3.9 %collective-permute-done = bf16[8,128,128]{2,1,0:T(8,128)(2,1)S(1)} collective-permute-done((bf16[8,128,128]{2,1,0:T(8,128)(2,1)S(1)}, bf16[8,128,128]{2,1,0:T(8,128)(2,1)S(1)}, u32[]{:S(2)}, u32[]{:S(2)}) %collective-permute-start) | collective-permute-done | bytes 262176 | tf_op jit(solution)/shard_map/while/body/eval_jaxpr/ppermute | solution.py:15
  39.2 0.7 multiply_reduce_fusion.1
  39.9 5.7 %psum.14 = f32[64]{0:T(128)S(1)} all-reduce(f32[64]{0:T(128)S(1)} %get-tuple-element.57), channel_id=1, replica_groups=mesh['groups'=2,'seq'=4,'exp'=2,'rep'=2] {'exp','rep'}, use_global_device_ids=true, to_apply=%region_4.5 | all-reduce | flops 64 | bytes 512 | tf_op jit(solution)/shard_map/psum | solution.py:88
  45.6 0.2 multiply_reduce_fusion
  45.9 6.6 %psum.15 = f32[64]{0:T(128)S(1)} all-reduce(f32[64]{0:T(128)S(1)} %get-tuple-element.53), channel_id=1, replica_groups=mesh['groups'=2,'seq'=4,'exp'=2,'rep'=2] {'exp','rep'}, use_global_device_ids=true, to_apply=%region_9.10 | all-reduce | flops 64 | bytes 512 | tf_op jit(solution)/shard_map/psum | solution.py:93
  52.6 0.1 eq.47
  52.8 0.2 reduce_window_sum.23
  53.1 0.2 eq.51
  53.3 0.2 eq.52
  53.5 0.2 mul.105
  53.7 0.2 mul.106
  54.0 0.2 fusion.68
  54.2 0.2 convolution_convert_fusion
  54.5 6.3 %all_to_all.30 = bf16[4,3,1024]{2,1,0:T(4,128)(2,1)S(1)} all-to-all(bf16[4,3,1024]{2,1,0:T(4,128)(2,1)S(1)} %reshape.149), channel_id=1, replica_groups=mesh['groups'=2,'seq'=4,'exp'=2,'rep'=2] {'exp','rep'}, dimensions={0} | all-to-all | bytes 49152 | tf_op jit(solution)/shard_map/all_to_all | solution.py:105
  60.8 14.6 %all-gather = bf16[4,3,4096]{2,1,0:T(4,128)(2,1)S(1)} all-gather(bf16[1,3,4096]{2,1,0:T(4,128)(2,1)S(1)} %bitcast.105), channel_id=1, replica_groups=mesh['groups'=2,'seq'=4,'exp'=2,'rep'=2] {'seq'}, dimensions={0}, use_global_device_ids=true | all-gather | bytes 122880 | tf_op jit(solution)/shard_map/all_gather | solution.py:110
  75.4 6.2 %fusion.6 = f32[12,1152]{1,0:T(8,128)S(1)} fusion(bf16[12,4096]{1,0:T(8,128)(2,1)S(1)} %reshape.154, bf16[1,1152,4096]{2,1,0:T(8,128)(2,1)} %param.25), kind=kOutput, calls=%fused_computation.7 | convolution fusion | flops 113246208 | bytes 9590784 | tf_op jit(solution)/shard_map/dot_general | solution.py:35
  81.7 11.4 %fusion.8 = bf16[12,4096]{1,0:T(8,128)(2,1)} fusion(bf16[1,1152,4096]{2,1,0:T(8,128)(2,1)} %param.27, bf16[12,4096]{1,0:T(8,128)(2,1)S(1)} %reshape.154, bf16[1,1152,4096]{2,1,0:T(8,128)(2,1)} %param.26, f32[12,1152]{1,0:T(8,128)S(1)} %fusion.6), kind=kOutput, calls=%fused_computation.9 | convolution fusion | flops 226624512 | bytes 19126272 | tf_op jit(solution)/shard_map/dot_general | solution.py:114
  93.1 0.6 dynamic-slice
  94.2 33.9 %all-reduce.3.cloned.1.call-done = bf16[12,4096]{1,0:T(8,128)(2,1)} async-done(((bf16[12,4096]{1,0:T(8,128)(2,1)}), bf16[12,4096]{1,0:T(8,128)(2,1)}) %all-reduce.3.cloned.1.call-update) | async-done | bytes 98320
  128.2 0.9 constant_dynamic-slice_fusion
  129.1 6.5 %all_to_all.31 = bf16[3,4,1024]{2,0,1:T(4,128)(2,1)S(1)} all-to-all(bf16[3,4,1024]{2,0,1:T(4,128)(2,1)S(1)} %bitcast.106), channel_id=1, replica_groups=mesh['groups'=2,'seq'=4,'exp'=2,'rep'=2] {'exp','rep'}, dimensions={1} | all-to-all | bytes 49152 | tf_op jit(solution)/shard_map/all_to_all | solution.py:123
  135.6 0.9 fusion.19
  (45 shorter events, 1.4 us)
Async XLA Ops:
  6.5 1.3 copy-start
  6.5 32.7 %copy-start.1 = (bf16[64,1024]{1,0:T(8,128)(2,1)S(1)}, bf16[64,1024]{1,0:T(8,128)(2,1)}, u32[]{:S(2)}) copy-start(bf16[64,1024]{1,0:T(8,128)(2,1)} %param.15) | copy-start | bytes 393220
  6.5 39.1 %copy-start.3 = (bf16[64,1024]{1,0:T(8,128)(2,1)S(1)}, bf16[64,1024]{1,0:T(8,128)(2,1)}, u32[]{:S(2)}) copy-start(bf16[64,1024]{1,0:T(8,128)(2,1)} %param.19) | copy-start | bytes 393220
  6.5 39.1 %copy-start.2 = (bf16[64,1024]{1,0:T(8,128)(2,1)S(1)}, bf16[64,1024]{1,0:T(8,128)(2,1)}, u32[]{:S(2)}) copy-start(bf16[64,1024]{1,0:T(8,128)(2,1)} %param.20) | copy-start | bytes 393220
  6.5 39.1 %copy-start.4 = (f32[1024]{0:T(1024)S(1)}, f32[1024]{0:T(1024)}, u32[]{:S(2)}) copy-start(f32[1024]{0:T(1024)} %param.21) | copy-start | bytes 12292
  6.5 46.0 %copy-start.6 = (s32[64,2]{0,1:T(2,128)S(1)}, s32[64,2]{0,1:T(2,128)}, u32[]{:S(2)}) copy-start(s32[64,2]{0,1:T(2,128)} %param.23) | copy-start | bytes 1540
  6.6 47.3 %copy-start.7 = (f32[64,2]{0,1:T(2,128)S(1)}, f32[64,2]{0,1:T(2,128)}, u32[]{:S(2)}) copy-start(f32[64,2]{0,1:T(2,128)} %param.24) | copy-start | bytes 1540
  6.6 47.7 %copy-start.5 = (f32[1024]{0:T(1024)S(1)}, f32[1024]{0:T(1024)}, u32[]{:S(2)}) copy-start(f32[1024]{0:T(1024)} %param.22) | copy-start | bytes 12292
  6.6 121.6 %all-reduce.3.cloned.1.call-start = ((), (), s32[]{:S(2)}) async-start(), calls=%async_computation.2 | async-start | bytes 262144
  10.9 10.5 %collective-permute-start = (bf16[8,128,128]{2,1,0:T(8,128)(2,1)S(1)}, bf16[8,128,128]{2,1,0:T(8,128)(2,1)S(1)}, u32[]{:S(2)}, u32[]{:S(2)}) collective-permute-start(bf16[8,128,128]{2,1,0:T(8,128)(2,1)S(1)} %fusion.88), channel_id=1, source_target_pairs={{0,4},{4,8},{8,12},{1,5},{5,9},{9,13},{2,6},{6,10},{10,14},{3,7},{... | collective-permute-start | bytes 786440 | tf_op jit(solution)/shard_map/while/body/eval_jaxpr/ppermute | solution.py:15
  21.6 9.1 %collective-permute-start = (bf16[8,128,128]{2,1,0:T(8,128)(2,1)S(1)}, bf16[8,128,128]{2,1,0:T(8,128)(2,1)S(1)}, u32[]{:S(2)}, u32[]{:S(2)}) collective-permute-start(bf16[8,128,128]{2,1,0:T(8,128)(2,1)S(1)} %fusion.88), channel_id=1, source_target_pairs={{0,4},{4,8},{8,12},{1,5},{5,9},{9,13},{2,6},{6,10},{10,14},{3,7},{... | collective-permute-start | bytes 786440 | tf_op jit(solution)/shard_map/while/body/eval_jaxpr/ppermute | solution.py:15
  30.9 8.3 %collective-permute-start = (bf16[8,128,128]{2,1,0:T(8,128)(2,1)S(1)}, bf16[8,128,128]{2,1,0:T(8,128)(2,1)S(1)}, u32[]{:S(2)}, u32[]{:S(2)}) collective-permute-start(bf16[8,128,128]{2,1,0:T(8,128)(2,1)S(1)} %fusion.88), channel_id=1, source_target_pairs={{0,4},{4,8},{8,12},{1,5},{5,9},{9,13},{2,6},{6,10},{10,14},{3,7},{... | collective-permute-start | bytes 786440 | tf_op jit(solution)/shard_map/while/body/eval_jaxpr/ppermute | solution.py:15
  81.7 11.4 %copy-start.8 = (u32[32]{0:T(128)S(1)}, u32[32]{0:T(128)}, u32[]{:S(2)}) copy-start(u32[32]{0:T(128)} %constant.31) | copy-start | bytes 388
Sparse Core Ops, SparseCore 0:
  93.2 34.9 all-reduce.2
where the time goes:
time: 144 us; the launch traced here: 143 us
  waiting for transfers between devices  48 us (33%)
  blocking collectives  39.6 us (28%)
  matrix products  22.3 us (15%)
  between operations  14.1 us (10%)
  starting transfers between devices  13.8 us (10%)
  local copies, waits for them, and re-layouts  3.89 us (3%)
  other arithmetic  1.46 us (1%)
    unnamed x2, waiting for transfers between devices  34 us
    all_gather x1, blocking collectives, shards(): gathered = lax.all_gather(rows_local, 'seq', axis=0, tiled=True)  14.6 us
    ppermute x3, waiting for transfers between devices, from_behind(): return lax.ppermute(block, axis, route)  14.1 us
    ppermute x3, starting transfers between devices, from_behind(): return lax.ppermute(block, axis, route)  13.8 us
    dot_general x1, matrix products, shards(): jnp.dot((jax.nn.silu(gate_val) * up_val).astype(jnp.bfloat16), down_mat,...  11.4 us
    psum x1, blocking collectives, shards(): moe_sumsq = lax.psum(jnp.sum(hidden * hidden, axis=1), ('exp', 'rep'))  6.61 us
    all_to_all x1, blocking collectives, shards(): lax.all_to_all(summed.reshape(half_cap, column_groups, columns), ('exp',...  6.47 us
    all_to_all x1, blocking collectives, shards(): lax.all_to_all(packed, ('exp', 'rep'), split_axis=0, concat_axis=2, tiled...  6.3 us
  transfers between devices with their start and end apart: 4, of which 4 were waited for; matrix products, arithmetic and copies ran while one was open for 0% of the time, Pallas kernels for 0%

commit v1 on v0

v1 whole, which is shorter than its diff:
```python
import jax
import jax.numpy as jnp
from jax import lax
from jax.experimental import pallas as pl
from jax.experimental.pallas import tpu as pltpu
from jax.sharding import PartitionSpec as P

CAP = 6
SLOTS = 8
EPSILON = 1e-06
MESH = pl.DeviceIdType.MESH
F32 = jnp.float32
BF16 = jnp.bfloat16


def sweep(count, body):
    if count <= 16:
        for i in range(count):
            body(i)
    else:
        lax.fori_loop(0, count, lambda i, c: (body(i), c)[1], 0)


def nt_dot(a, b):
    return lax.dot_general(a, b, (((1,), (1,)), ((), ())), preferred_element_type=F32)


def kernel(
    n_seq,
    n_exp,
    n_rep,
    q_ref,
    k_ref,
    v_ref,
    decay_ref,
    res_ref,
    gate_ref,
    again_ref,
    mgain_ref,
    routes_ref,
    rw_ref,
    wg_hbm,
    wu_hbm,
    wd_hbm,
    out_ref,
    wg,
    wu,
    wd,
    state_in,
    state_out,
    block_state,
    att,
    u_buf,
    sums,
    pack,
    rows,
    xbig,
    half_send,
    half_recv,
    fin,
    back,
    w_sem,
    chain_send,
    chain_recv,
    sums_send,
    sums_recv,
    disp_send,
    disp_recv,
    swap_send,
    swap_recv,
    half_ssem,
    half_rsem,
    back_send,
    back_recv,
):
    z = lax.axis_index("seq")
    x = lax.axis_index("exp")
    r = lax.axis_index("rep")
    other = 1 - r
    tokens, columns = q_ref.shape
    heads = decay_ref.shape[1]
    hd = columns // heads
    hidden_rows = wg.shape[0]
    width = columns * n_exp * n_rep
    whole_rows = wg_hbm.shape[1]

    first = pl.multiple_of(r * hidden_rows, 16) if hidden_rows != whole_rows else 0
    loads = [
        pltpu.make_async_copy(src.at[0, pl.ds(first, hidden_rows), :], dst, w_sem.at[i])
        for i, (src, dst) in enumerate(((wg_hbm, wg), (wu_hbm, wu), (wd_hbm, wd)))
    ]
    for load in loads:
        load.start()

    barrier = pltpu.get_barrier_semaphore()
    plane = n_exp * n_seq

    def greet(i):
        j = i + 1
        pl.semaphore_signal(
            barrier,
            inc=1,
            device_id={
                "exp": lax.rem(x + lax.rem(j, n_exp), n_exp),
                "seq": lax.rem(z + lax.div(j, n_exp), n_seq),
                "rep": r,
            },
            device_id_type=MESH,
        )

    sweep(plane - 1, greet)
    for e in range(n_exp):
        pl.semaphore_signal(
            barrier,
            inc=1,
            device_id={"exp": e, "seq": z, "rep": other},
            device_id_type=MESH,
        )

    ti = lax.broadcasted_iota(jnp.int32, (tokens, tokens), 0)
    tj = lax.broadcasted_iota(jnp.int32, (tokens, tokens), 1)
    causal = ti >= tj
    tri = jnp.where(causal, 1.0, 0.0).astype(F32)
    decay = decay_ref[...]
    cum = jnp.dot(tri, decay, precision=lax.Precision.HIGHEST, preferred_element_type=F32)
    cum_t = jnp.transpose(cum)
    ending = cum[tokens - 1 : tokens, :]
    fading = jnp.exp(ending)
    to_end = jnp.exp(ending - cum)
    lift = jnp.exp(cum)
    for h in range(heads):
        cols = slice(h * hd, (h + 1) * hd)
        faded = k_ref[:, cols].astype(F32) * to_end[:, h : h + 1]
        block_state[h] = jnp.dot(
            jnp.transpose(faded).astype(BF16), v_ref[:, cols], preferred_element_type=F32
        )

    @pl.when(z == 0)
    def _():
        state_in[...] = jnp.zeros_like(state_in)

    pl.semaphore_wait(barrier, plane - 1 + n_exp)

    def hop(h):
        return pltpu.make_async_remote_copy(
            src_ref=state_out.at[h],
            dst_ref=state_in.at[h],
            send_sem=chain_send.at[h],
            recv_sem=chain_recv.at[h],
            device_id={"seq": z + 1},
            device_id_type=MESH,
        )

    @pl.when(z == 0)
    def _():
        for h in range(heads):
            state_out[h] = block_state[h].astype(BF16)
            hop(h).start()

    for h in range(heads):
        cols = slice(h * hd, (h + 1) * hd)
        scores = nt_dot(q_ref[:, cols], k_ref[:, cols])
        gaps = cum[:, h : h + 1] - cum_t[h : h + 1, :]
        mixing = jnp.where(causal, scores * jnp.exp(jnp.where(causal, gaps, 0.0)), 0.0)
        att[:, cols] = jnp.dot(mixing.astype(BF16), v_ref[:, cols], preferred_element_type=F32)

    lane = lax.broadcasted_iota(jnp.int32, (tokens, 128), 1)
    expert_of = lax.div(lane, SLOTS)
    slot_of = lax.rem(lane, SLOTS)
    first_hit = routes_ref[:, 0:1] == expert_of
    second_hit = routes_ref[:, 1:2] == expert_of
    hit = jnp.where(first_hit | second_hit, 1.0, 0.0)
    strict = jnp.where(ti > tj, 1.0, 0.0).astype(BF16)
    before = jnp.dot(strict, hit.astype(BF16), preferred_element_type=F32)
    taken = (hit > 0.5) & (before.astype(jnp.int32) == slot_of) & (slot_of < CAP)
    onehot = jnp.where(taken, 1.0, 0.0)
    combine = jnp.where(first_hit, rw_ref[:, 0:1], rw_ref[:, 1:2]) * onehot
    dispatch = jnp.transpose(onehot)[0 : n_exp * SLOTS, :].astype(BF16)

    for h in range(heads):
        cols = slice(h * hd, (h + 1) * hd)

        @pl.when(z > 0)
        def _():
            hop(h).wait_recv()

            @pl.when(z < n_seq - 1)
            def _():
                state_out[h] = (
                    fading[:, h : h + 1] * state_in[h].astype(F32) + block_state[h]
                ).astype(BF16)
                hop(h).start()

            lifted = (q_ref[:, cols].astype(F32) * lift[:, h : h + 1]).astype(BF16)
            att[:, cols] += jnp.dot(lifted, state_in[h], preferred_element_type=F32)

    res = res_ref[...].astype(F32)
    attended = att[...]
    u = jax.nn.sigmoid(gate_ref[...].astype(F32)) * attended * again_ref[...]
    u_buf[...] = u
    parts = (attended * attended, res * u, u * u, res * res)
    table = jnp.zeros((tokens, 128), F32)
    for i, part in enumerate(parts):
        table = jnp.where(lane == i, jnp.sum(part, axis=1, keepdims=True), table)
    peers = n_exp * n_rep
    me = x * n_rep + r
    sums[me] = jnp.transpose(table)[0:8, :]

    def tell(i):
        to = lax.rem(me + 1 + i, peers)
        pltpu.make_async_remote_copy(
            src_ref=sums.at[me],
            dst_ref=sums.at[me],
            send_sem=sums_send,
            recv_sem=sums_recv,
            device_id={"exp": lax.div(to, n_rep), "rep": lax.rem(to, n_rep)},
            device_id_type=MESH,
        ).start()

    sweep(peers - 1, tell)
    many = sums.at[pl.ds(0, peers - 1)]
    pltpu.make_async_copy(many, many, sums_recv).wait()
    total = jnp.sum(sums[...], axis=0)
    s1 = lax.rsqrt(total[0:1, :] / width + EPSILON)
    moe = total[3:4, :] + s1 * (2.0 * total[1:2, :] + s1 * total[2:3, :])
    s2 = lax.rsqrt(jnp.maximum(moe, 0.0) / width + EPSILON)
    row8 = lax.broadcasted_iota(jnp.int32, (8, tokens), 0)
    scales = jnp.transpose(jnp.where(row8 == 0, s1, s2))
    hidden = res_ref[...].astype(F32) + scales[:, 0:1] * u_buf[...]
    u_buf[...] = hidden
    normed = (hidden * scales[:, 1:2] * mgain_ref[...]).astype(BF16)

    packed = jnp.dot(dispatch, normed, preferred_element_type=F32)
    for e in range(n_exp):
        pack[e] = packed[e * SLOTS : (e + 1) * SLOTS, :].astype(BF16)
    here = x * n_seq + z
    rows[r, here] = pack[x]

    def place(i):
        j = plane - 1 - i
        e = lax.rem(x + lax.rem(j, n_exp), n_exp)
        to = lax.rem(z + lax.div(j, n_exp), n_seq)
        return e, to

    def deal(i):
        e, to = place(i)
        pltpu.make_async_remote_copy(
            src_ref=pack.at[e],
            dst_ref=rows.at[r, here],
            send_sem=disp_send,
            recv_sem=disp_recv,
            device_id={"exp": e, "seq": to},
            device_id_type=MESH,
        ).start()

    sweep(plane - 1, deal)
    arrived = rows.at[r, pl.ds(0, plane - 1)]
    pltpu.make_async_copy(arrived, arrived, disp_recv).wait()
    swap = pltpu.make_async_remote_copy(
        src_ref=rows.at[r],
        dst_ref=rows.at[r],
        send_sem=swap_send,
        recv_sem=swap_recv,
        device_id={"rep": other},
        device_id_type=MESH,
    )
    swap.start()
    for load in loads:
        load.wait()
    slots = n_seq * SLOTS
    swap.wait()
    for s in range(n_rep):
        for e in range(n_exp):
            chunk = rows[s, pl.ds(e * n_seq, n_seq)].astype(F32).reshape(slots, columns)
            at = (e * n_rep + s) * columns
            xbig[:, at : at + columns] = chunk.astype(BF16)

    gate_val = nt_dot(wg[...], xbig[...])
    up_val = nt_dot(wu[...], xbig[...])
    inner = gate_val / (1.0 + jnp.exp(-gate_val)) * up_val
    if hidden_rows == whole_rows:
        unit = lax.broadcasted_iota(jnp.int32, inner.shape, 0)
        inner = jnp.where(lax.div(unit, whole_rows // n_rep) == r, inner, 0.0)
    inner = jnp.transpose(inner).astype(BF16)

    def product(e, s):
        at = pl.multiple_of((e * n_rep + s) * columns, 128)
        return jnp.dot(inner, wd[:, pl.ds(at, columns)], preferred_element_type=F32)

    def half(e):
        return pltpu.make_async_remote_copy(
            src_ref=half_send.at[e],
            dst_ref=half_recv.at[e],
            send_sem=half_ssem.at[e],
            recv_sem=half_rsem.at[e],
            device_id={"rep": other},
            device_id_type=MESH,
        )

    for e in range(n_exp):
        half_send[e] = product(e, other).astype(BF16)
        half(e).start()

    here_back = x * n_seq + z
    for e in range(n_exp):
        own = product(e, r)
        half(e).wait_recv()
        whole = (own + half_recv[e].astype(F32)).reshape(n_seq, SLOTS, columns)
        fin[pl.ds(e * n_seq, n_seq)] = whole.astype(BF16)

    back[here_back] = fin[here_back]

    def hand_back(i):
        e, to = place(i)
        pltpu.make_async_remote_copy(
            src_ref=fin.at[e * n_seq + to],
            dst_ref=back.at[here_back],
            send_sem=back_send,
            recv_sem=back_recv,
            device_id={"exp": e, "seq": to},
            device_id_type=MESH,
        ).start()

    sweep(plane - 1, hand_back)
    returned = back.at[pl.ds(0, plane - 1)]
    pltpu.make_async_copy(returned, returned, back_recv).wait()
    coarse = combine.astype(BF16)
    fine = (combine - coarse.astype(F32)).astype(BF16)
    result = u_buf[...]
    for e in range(n_exp):
        rows_e = jnp.sum(back[pl.ds(e * n_seq, n_seq)].astype(F32), axis=0).astype(BF16)
        lanes = slice(e * SLOTS, (e + 1) * SLOTS)
        result += jnp.dot(coarse[:, lanes], rows_e, preferred_element_type=F32)
        result += jnp.dot(fine[:, lanes], rows_e, preferred_element_type=F32)
    out_ref[...] = result.astype(BF16)

    for h in range(heads):

        @pl.when(z < n_seq - 1)
        def _():
            hop(h).wait_send()

    pltpu.make_async_copy(many, many, sums_send).wait()
    pltpu.make_async_copy(arrived, arrived, disp_send).wait()
    for e in range(n_exp):
        half(e).wait_send()
    pltpu.make_async_copy(returned, returned, back_send).wait()


def solution(mesh):
    n_seq, n_exp, n_rep = (mesh.shape[a] for a in ("seq", "exp", "rep"))

    def shards(
        queries,
        key_rows,
        value_rows,
        decay_log,
        residual,
        out_gate,
        attn_gain,
        moe_gain,
        routes,
        route_weights,
        w_gate,
        w_up,
        w_down,
    ):
        tokens, columns = queries.shape
        heads = decay_log.shape[1]
        hd = columns // heads
        _, whole_rows, width = w_gate.shape
        even = whole_rows % (16 * n_rep) == 0
        hidden_rows = whole_rows // n_rep if even else whole_rows
        plane = n_exp * n_seq
        slots = n_seq * SLOTS
        vmem = pl.BlockSpec(memory_space=pltpu.VMEM)
        hbm = pl.BlockSpec(memory_space=pltpu.HBM)
        dma = pltpu.SemaphoreType.DMA
        return pl.pallas_call(
            lambda *refs: kernel(n_seq, n_exp, n_rep, *refs),
            name="layer",
            out_shape=jax.ShapeDtypeStruct((tokens, columns), BF16),
            in_specs=[vmem] * 10 + [hbm] * 3,
            out_specs=vmem,
            scratch_shapes=[
                pltpu.VMEM((hidden_rows, width), BF16),
                pltpu.VMEM((hidden_rows, width), BF16),
                pltpu.VMEM((hidden_rows, width), BF16),
                pltpu.VMEM((heads, hd, hd), BF16),
                pltpu.VMEM((heads, hd, hd), BF16),
                pltpu.VMEM((heads, hd, hd), F32),
                pltpu.VMEM((tokens, columns), F32),
                pltpu.VMEM((tokens, columns), F32),
                pltpu.VMEM((n_exp * n_rep, 8, tokens), F32),
                pltpu.VMEM((n_exp, SLOTS, columns), BF16),
                pltpu.VMEM((n_rep, plane, SLOTS, columns), BF16),
                pltpu.VMEM((slots, width), BF16),
                pltpu.VMEM((n_exp, slots, columns), BF16),
                pltpu.VMEM((n_exp, slots, columns), BF16),
                pltpu.VMEM((plane, SLOTS, columns), BF16),
                pltpu.VMEM((plane, SLOTS, columns), BF16),
                dma((3,)),
                dma((heads,)),
                dma((heads,)),
                dma,
                dma,
                dma,
                dma,
                dma,
                dma,
                dma((n_exp,)),
                dma((n_exp,)),
                dma,
                dma,
            ],
            compiler_params=pltpu.CompilerParams(collective_id=0, has_side_effects=True),
        )(
            queries,
            key_rows,
            value_rows,
            decay_log,
            residual,
            out_gate,
            attn_gain.reshape(1, columns),
            moe_gain.reshape(1, columns),
            routes,
            route_weights,
            w_gate,
            w_up,
            w_down,
        )

    block = P(("groups", "seq"), ("exp", "rep"))
    gain = P(("exp", "rep"))
    route = P(("groups", "seq"), None)
    weight = P("exp", "seq", None)
    return jax.shard_map(
        shards,
        mesh=mesh,
        in_specs=(block,) * 6 + (gain, gain, route, route) + (weight,) * 3,
        out_specs=block,
        check_vma=False,
    )
```

time: 144 us -> 47.1 us (0.33)
  waiting for transfers between devices: 48 us -> 0 us
  Pallas kernels: 0 us -> 41.2 us
  blocking collectives: 39.6 us -> 0 us
  matrix products: 22.3 us -> 0 us
  between operations: 14.1 us -> 0.01 us
  starting transfers between devices: 13.8 us -> 0 us
  local copies, waits for them, and re-layouts: 3.89 us -> 5.69 us
  other arithmetic: 1.46 us -> 0 us
    pallas_call x0 -> x1, Pallas kernels: none -> 41.2 us  [shards(): pl.pallas_call(lambda *refs: kernel(n_seq, n_exp, n_rep, *refs), name='la...]
    unnamed x2 -> x0, waiting for transfers between devices: 34 us -> none
    dot_general x7 -> x0, matrix products: 22.3 us -> none  [the longest x1 11.4 us: shards(): jnp.dot((jax.nn.silu(gate_val) * up_val).astype(jnp.bfloat16), down_mat,...]
    all_gather x1 -> x0, blocking collectives: 14.6 us -> none  [shards(): gathered = lax.all_gather(rows_local, 'seq', axis=0, tiled=True)]
    ppermute x3 -> x0, waiting for transfers between devices: 14.1 us -> none  [from_behind(): return lax.ppermute(block, axis, route)]
    ppermute x3 -> x0, starting transfers between devices: 13.8 us -> none  [from_behind(): return lax.ppermute(block, axis, route)]
    all_to_all x2 -> x0, blocking collectives: 12.8 us -> none  [the longest x1 6.47 us: shards(): lax.all_to_all(summed.reshape(half_cap, column_groups, columns), ('exp',...]
    psum x2 -> x0, blocking collectives: 12.3 us -> none  [the longest x1 6.61 us: shards(): moe_sumsq = lax.psum(jnp.sum(hidden * hidden, axis=1), ('exp', 'rep'))]
  transfers between devices with their start and end apart: 4 -> 0, of which waited for: 4 -> 0; matrix products, arithmetic and copies ran while one was open for 0% -> 0% of each run, Pallas kernels for 0% -> 0%
where the time goes in v1:
time: 47.1 us; the launch traced here: 46.9 us
  Pallas kernels  41.2 us (87%)
  local copies, waits for them, and re-layouts  5.69 us (12%)
    pallas_call x1, Pallas kernels, shards(): pl.pallas_call(lambda *refs: kernel(n_seq, n_exp, n_rep, *refs), name='la...  41.2 us
    unnamed x4, local copies, waits for them, and re-layouts  5.69 us

profile of v1, /device:TPU:0, one launch (start us, length us, event | category | flops | bytes accessed | tf_op | source)
XLA Modules:
  0.0 46.9 jit_solution(16868937105171466391)
XLA Ops:
  0.0 1.4 %copy.14.refs_3_ = f32[64,8]{1,0:T(8,128)} copy(f32[64,8]{0,1:T(8,128)} %param.16) | data formatting | bytes 4096 | tf_op args[3]
  1.4 1.4 %copy.15.refs_8_ = s32[64,2]{1,0:T(8,128)} copy(s32[64,2]{0,1:T(2,128)} %param.21) | data formatting | bytes 1024 | tf_op args[8]
  2.7 1.4 %copy.16.refs_9_ = f32[64,2]{1,0:T(8,128)} copy(f32[64,2]{0,1:T(2,128)} %param.22) | data formatting | bytes 1024 | tf_op args[9]
  4.1 41.2 %layer.1 = bf16[64,1024]{1,0:T(8,128)(2,1)} custom-call(bf16[64,1024]{1,0:T(8,128)(2,1)} %refs_0_.1, bf16[64,1024]{1,0:T(8,128)(2,1)} %refs_1_.1, bf16[64,1024]{1,0:T(8,128)(2,1)} %refs_2_.1, f32[64,8]{1,0:T(8,128)} %copy.14.refs_3_, bf16[64,1024]{1,0:T(8,128)(2,1)} %refs_4_.1, bf16[64,1024]{1,0:T(8,128)(2,1)} %refs_5_.1, f32[1,1024]{1,0:T(1,128)} %bitcast.2, ...), custom_call_target="tpu_custom_call" | custom-call | tf_op jit(solution)/shard_map/layer/pallas_call | solution.py:379
  45.3 1.6 %copy.18 = bf16[64,1024]{1,0:T(8,128)(2,1)} copy(bf16[64,1024]{1,0:T(8,128)(2,1)} %layer.1) | data formatting | bytes 262144

commit v2 on v1

--- a/solution.py
+++ b/solution.py
@@ -7,6 +7,7 @@
 
 CAP = 6
 SLOTS = 8
+PARTS = 2
 EPSILON = 1e-06
 MESH = pl.DeviceIdType.MESH
 F32 = jnp.float32
@@ -29,20 +30,30 @@
     n_seq,
     n_exp,
     n_rep,
-    q_ref,
+    k_hbm,
+    v_hbm,
+    decay_hbm,
+    q_hbm,
+    routes_hbm,
+    rw_hbm,
+    res_hbm,
+    gate_hbm,
+    again_hbm,
+    mgain_hbm,
+    wg_hbm,
+    wu_hbm,
+    wd_hbm,
+    out_ref,
     k_ref,
     v_ref,
     decay_ref,
+    q_ref,
+    routes_ref,
+    rw_ref,
     res_ref,
     gate_ref,
     again_ref,
     mgain_ref,
-    routes_ref,
-    rw_ref,
-    wg_hbm,
-    wu_hbm,
-    wd_hbm,
-    out_ref,
     wg,
     wu,
     wd,
@@ -54,12 +65,14 @@
     sums,
     pack,
     rows,
-    xbig,
     half_send,
     half_recv,
     fin,
     back,
+    in_sem,
     w_sem,
+    up_sem,
+    go_sem,
     chain_send,
     chain_recv,
     sums_send,
@@ -78,52 +91,73 @@
     r = lax.axis_index("rep")
     other = 1 - r
     tokens, columns = q_ref.shape
-    heads = decay_ref.shape[1]
+    heads = decay_ref.shape[0]
     hd = columns // heads
+    part_rows = hd // PARTS
     hidden_rows = wg.shape[0]
     width = columns * n_exp * n_rep
     whole_rows = wg_hbm.shape[1]
 
+    inputs = [
+        pltpu.make_async_copy(src, dst, in_sem.at[i])
+        for i, (src, dst) in enumerate(
+            (
+                (k_hbm, k_ref),
+                (v_hbm, v_ref),
+                (decay_hbm, decay_ref),
+                (q_hbm, q_ref),
+                (routes_hbm, routes_ref),
+                (rw_hbm, rw_ref),
+                (res_hbm, res_ref),
+                (gate_hbm, gate_ref),
+                (again_hbm, again_ref),
+                (mgain_hbm, mgain_ref),
+            )
+        )
+    ]
+    for load in inputs:
+        load.start()
     first = pl.multiple_of(r * hidden_rows, 16) if hidden_rows != whole_rows else 0
     loads = [
         pltpu.make_async_copy(src.at[0, pl.ds(first, hidden_rows), :], dst, w_sem.at[i])
         for i, (src, dst) in enumerate(((wg_hbm, wg), (wu_hbm, wu), (wd_hbm, wd)))
     ]
+
+    barrier = pltpu.get_barrier_semaphore()
+    plane = n_exp * n_seq
+    peers = n_exp * n_rep
+    me = x * n_rep + r
+    last = n_seq - 1
+
+    def greet(where):
+        pl.semaphore_signal(barrier, inc=1, device_id=where, device_id_type=MESH)
+
+    @pl.when(z < last)
+    def _():
+        greet({"seq": z + 1})
+
+    @pl.when(z > 0)
+    def _():
+        greet({"seq": z - 1})
+
+    def greet_peer(i):
+        to = lax.rem(me + 1 + i, peers)
+        greet({"exp": lax.div(to, n_rep), "rep": lax.rem(to, n_rep)})
+
+    sweep(peers - 1, greet_peer)
     for load in loads:
         load.start()
-
-    barrier = pltpu.get_barrier_semaphore()
-    plane = n_exp * n_seq
-
-    def greet(i):
-        j = i + 1
-        pl.semaphore_signal(
-            barrier,
-            inc=1,
-            device_id={
-                "exp": lax.rem(x + lax.rem(j, n_exp), n_exp),
-                "seq": lax.rem(z + lax.div(j, n_exp), n_seq),
-                "rep": r,
-            },
-            device_id_type=MESH,
-        )
-
-    sweep(plane - 1, greet)
-    for e in range(n_exp):
-        pl.semaphore_signal(
-            barrier,
-            inc=1,
-            device_id={"exp": e, "seq": z, "rep": other},
-            device_id_type=MESH,
-        )
+    for load in inputs[:3]:
+        load.wait()
 
     ti = lax.broadcasted_iota(jnp.int32, (tokens, tokens), 0)
     tj = lax.broadcasted_iota(jnp.int32, (tokens, tokens), 1)
     causal = ti >= tj
-    tri = jnp.where(causal, 1.0, 0.0).astype(F32)
-    decay = decay_ref[...]
-    cum = jnp.dot(tri, decay, precision=lax.Precision.HIGHEST, preferred_element_type=F32)
-    cum_t = jnp.transpose(cum)
+    upper = jnp.where(tj >= ti, 1.0, 0.0).astype(F32)
+    cum_t = jnp.dot(
+        decay_ref[...], upper, precision=lax.Precision.HIGHEST, preferred_element_type=F32
+    )
+    cum = jnp.transpose(cum_t)
     ending = cum[tokens - 1 : tokens, :]
     fading = jnp.exp(ending)
     to_end = jnp.exp(ending - cum)
@@ -135,18 +169,16 @@
             jnp.transpose(faded).astype(BF16), v_ref[:, cols], preferred_element_type=F32
         )
 
-    @pl.when(z == 0)
-    def _():
-        state_in[...] = jnp.zeros_like(state_in)
-
-    pl.semaphore_wait(barrier, plane - 1 + n_exp)
-
-    def hop(h):
+    ends = (z > 0).astype(jnp.int32) + (z < last).astype(jnp.int32)
+    pl.semaphore_wait(barrier, peers - 1 + ends)
+
+    def hop(h, p):
+        piece = pl.ds(p * part_rows, part_rows)
         return pltpu.make_async_remote_copy(
-            src_ref=state_out.at[h],
-            dst_ref=state_in.at[h],
-            send_sem=chain_send.at[h],
-            recv_sem=chain_recv.at[h],
+            src_ref=state_out.at[h, piece],
+            dst_ref=state_in.at[h, piece],
+            send_sem=chain_send.at[h, p],
+            recv_sem=chain_recv.at[h, p],
             device_id={"seq": z + 1},
             device_id_type=MESH,
         )
@@ -155,7 +187,17 @@
     def _():
         for h in range(heads):
             state_out[h] = block_state[h].astype(BF16)
-            hop(h).start()
+            for p in range(PARTS):
+                hop(h, p).start()
+
+    def raise_hand():
+        pl.semaphore_signal(up_sem, inc=1, device_id={"seq": z - 1}, device_id_type=MESH)
+
+    @pl.when(z == last)
+    def _():
+        raise_hand()
+
+    inputs[3].wait()
 
     for h in range(heads):
         cols = slice(h * hd, (h + 1) * hd)
@@ -164,35 +206,59 @@
         mixing = jnp.where(causal, scores * jnp.exp(jnp.where(causal, gaps, 0.0)), 0.0)
         att[:, cols] = jnp.dot(mixing.astype(BF16), v_ref[:, cols], preferred_element_type=F32)
 
+    @pl.when(z < last)
+    def _():
+        pl.semaphore_wait(up_sem, 1)
+
+        @pl.when(z > 0)
+        def _():
+            raise_hand()
+
+    for load in inputs[4:]:
+        load.wait()
     lane = lax.broadcasted_iota(jnp.int32, (tokens, 128), 1)
     expert_of = lax.div(lane, SLOTS)
     slot_of = lax.rem(lane, SLOTS)
-    first_hit = routes_ref[:, 0:1] == expert_of
-    second_hit = routes_ref[:, 1:2] == expert_of
+    named = jnp.transpose(routes_ref[...].astype(F32)).astype(jnp.int32)
+    shares = jnp.transpose(rw_ref[...])
+    first_hit = named[:, 0:1] == expert_of
+    second_hit = named[:, 1:2] == expert_of
     hit = jnp.where(first_hit | second_hit, 1.0, 0.0)
     strict = jnp.where(ti > tj, 1.0, 0.0).astype(BF16)
     before = jnp.dot(strict, hit.astype(BF16), preferred_element_type=F32)
     taken = (hit > 0.5) & (before.astype(jnp.int32) == slot_of) & (slot_of < CAP)
     onehot = jnp.where(taken, 1.0, 0.0)
-    combine = jnp.where(first_hit, rw_ref[:, 0:1], rw_ref[:, 1:2]) * onehot
+    combine = jnp.where(first_hit, shares[:, 0:1], shares[:, 1:2]) * onehot
     dispatch = jnp.transpose(onehot)[0 : n_exp * SLOTS, :].astype(BF16)
+
+    def let_go(i):
+        pl.semaphore_signal(go_sem, inc=1, device_id={"seq": i}, device_id_type=MESH)
 
     for h in range(heads):
         cols = slice(h * hd, (h + 1) * hd)
 
         @pl.when(z > 0)
         def _():
-            hop(h).wait_recv()
-
-            @pl.when(z < n_seq - 1)
-            def _():
-                state_out[h] = (
-                    fading[:, h : h + 1] * state_in[h].astype(F32) + block_state[h]
-                ).astype(BF16)
-                hop(h).start()
+            for p in range(PARTS):
+                piece = slice(p * part_rows, (p + 1) * part_rows)
+                hop(h, p).wait_recv()
+
+                @pl.when(z < last)
+                def _():
+                    state_out[h, piece] = (
+                        fading[:, h : h + 1] * state_in[h, piece].astype(F32)
+                        + block_state[h, piece]
+                    ).astype(BF16)
+                    hop(h, p).start()
 
             lifted = (q_ref[:, cols].astype(F32) * lift[:, h : h + 1]).astype(BF16)
             att[:, cols] += jnp.dot(lifted, state_in[h], preferred_element_type=F32)
+
+        if h == max(heads - 3, 0):
+
+            @pl.when(z == last)
+            def _():
+                sweep(last, let_go)
 
     res = res_ref[...].astype(F32)
     attended = att[...]
@@ -202,8 +268,6 @@
     table = jnp.zeros((tokens, 128), F32)
     for i, part in enumerate(parts):
         table = jnp.where(lane == i, jnp.sum(part, axis=1, keepdims=True), table)
-    peers = n_exp * n_rep
-    me = x * n_rep + r
     sums[me] = jnp.transpose(table)[0:8, :]
 
     def tell(i):
@@ -236,24 +300,49 @@
     here = x * n_seq + z
     rows[r, here] = pack[x]
 
-    def place(i):
-        j = plane - 1 - i
-        e = lax.rem(x + lax.rem(j, n_exp), n_exp)
-        to = lax.rem(z + lax.div(j, n_exp), n_seq)
-        return e, to
-
-    def deal(i):
-        e, to = place(i)
+    def deal(e, to, source, target, send_sem, recv_sem):
         pltpu.make_async_remote_copy(
-            src_ref=pack.at[e],
-            dst_ref=rows.at[r, here],
-            send_sem=disp_send,
-            recv_sem=disp_recv,
+            src_ref=source,
+            dst_ref=target,
+            send_sem=send_sem,
+            recv_sem=recv_sem,
             device_id={"exp": e, "seq": to},
             device_id_type=MESH,
         ).start()
 
-    sweep(plane - 1, deal)
+    def deal_rows(e, to):
+        deal(e, to, pack.at[e], rows.at[r, here], disp_send, disp_recv)
+
+    def earlier(send):
+        def one(i):
+            @pl.when(i < z)
+            def _():
+                for e in range(n_exp):
+                    send(e, i)
+
+        sweep(n_seq, one)
+
+    def level(send):
+        for j in range(1, n_exp):
+            send(lax.rem(x + j, n_exp), z)
+
+    def later(send):
+        def one(i):
+            @pl.when(last - i > z)
+            def _():
+                for e in range(n_exp):
+                    send(e, last - i)
+
+        sweep(n_seq, one)
+
+    earlier(deal_rows)
+    level(deal_rows)
+
+    @pl.when(z < last)
+    def _():
+        pl.semaphore_wait(go_sem, 1)
+
+    later(deal_rows)
     arrived = rows.at[r, pl.ds(0, plane - 1)]
     pltpu.make_async_copy(arrived, arrived, disp_recv).wait()
     swap = pltpu.make_async_remote_copy(
@@ -268,15 +357,22 @@
     for load in loads:
         load.wait()
     slots = n_seq * SLOTS
-    swap.wait()
-    for s in range(n_rep):
+
+    def project(s):
+        gate_part = up_part = 0.0
         for e in range(n_exp):
             chunk = rows[s, pl.ds(e * n_seq, n_seq)].astype(F32).reshape(slots, columns)
-            at = (e * n_rep + s) * columns
-            xbig[:, at : at + columns] = chunk.astype(BF16)
-
-    gate_val = nt_dot(wg[...], xbig[...])
-    up_val = nt_dot(wu[...], xbig[...])
+            chunk = chunk.astype(BF16)
+            at = pl.ds(pl.multiple_of((e * n_rep + s) * columns, 128), columns)
+            gate_part += nt_dot(wg[:, at], chunk)
+            up_part += nt_dot(wu[:, at], chunk)
+        return gate_part, up_part
+
+    gate_val, up_val = project(r)
+    swap.wait()
+    gate_part, up_part = project(other)
+    gate_val += gate_part
+    up_val += up_part
     inner = gate_val / (1.0 + jnp.exp(-gate_val)) * up_val
     if hidden_rows == whole_rows:
         unit = lax.broadcasted_iota(jnp.int32, inner.shape, 0)
@@ -310,18 +406,12 @@
 
     back[here_back] = fin[here_back]
 
-    def hand_back(i):
-        e, to = place(i)
-        pltpu.make_async_remote_copy(
-            src_ref=fin.at[e * n_seq + to],
-            dst_ref=back.at[here_back],
-            send_sem=back_send,
-            recv_sem=back_recv,
-            device_id={"exp": e, "seq": to},
-            device_id_type=MESH,
-        ).start()
-
-    sweep(plane - 1, hand_back)
+    def hand_back(e, to):
+        deal(e, to, fin.at[e * n_seq + to], back.at[here_back], back_send, back_recv)
+
+    earlier(hand_back)
+    later(hand_back)
+    level(hand_back)
     returned = back.at[pl.ds(0, plane - 1)]
     pltpu.make_async_copy(returned, returned, back_recv).wait()
     coarse = combine.astype(BF16)
@@ -336,9 +426,10 @@
 
     for h in range(heads):
 
-        @pl.when(z < n_seq - 1)
+        @pl.when(z < last)
         def _():
-            hop(h).wait_send()
+            for p in range(PARTS):
+                hop(h, p).wait_send()
 
     pltpu.make_async_copy(many, many, sums_send).wait()
     pltpu.make_async_copy(arrived, arrived, disp_send).wait()
@@ -380,9 +471,19 @@
             lambda *refs: kernel(n_seq, n_exp, n_rep, *refs),
             name="layer",
             out_shape=jax.ShapeDtypeStruct((tokens, columns), BF16),
-            in_specs=[vmem] * 10 + [hbm] * 3,
+            in_specs=[hbm] * 13,
             out_specs=vmem,
             scratch_shapes=[
+                pltpu.VMEM((tokens, columns), BF16),
+                pltpu.VMEM((tokens, columns), BF16),
+                pltpu.VMEM((heads, tokens), F32),
+                pltpu.VMEM((tokens, columns), BF16),
+                pltpu.VMEM((2, tokens), jnp.int32),
+                pltpu.VMEM((2, tokens), F32),
+                pltpu.VMEM((tokens, columns), BF16),
+                pltpu.VMEM((tokens, columns), BF16),
+                pltpu.VMEM((1, columns), F32),
+                pltpu.VMEM((1, columns), F32),
                 pltpu.VMEM((hidden_rows, width), BF16),
                 pltpu.VMEM((hidden_rows, width), BF16),
                 pltpu.VMEM((hidden_rows, width), BF16),
@@ -394,14 +495,16 @@
                 pltpu.VMEM((n_exp * n_rep, 8, tokens), F32),
                 pltpu.VMEM((n_exp, SLOTS, columns), BF16),
                 pltpu.VMEM((n_rep, plane, SLOTS, columns), BF16),
-                pltpu.VMEM((slots, width), BF16),
                 pltpu.VMEM((n_exp, slots, columns), BF16),
                 pltpu.VMEM((n_exp, slots, columns), BF16),
                 pltpu.VMEM((plane, SLOTS, columns), BF16),
                 pltpu.VMEM((plane, SLOTS, columns), BF16),
+                dma((10,)),
                 dma((3,)),
-                dma((heads,)),
-                dma((heads,)),
+                pltpu.SemaphoreType.REGULAR,
+                pltpu.SemaphoreType.REGULAR,
+                dma((heads, PARTS)),
+                dma((heads, PARTS)),
                 dma,
                 dma,
                 dma,
@@ -415,16 +518,16 @@
             ],
             compiler_params=pltpu.CompilerParams(collective_id=0, has_side_effects=True),
         )(
-            queries,
             key_rows,
             value_rows,
-            decay_log,
+            decay_log.T,
+            queries,
+            routes.T,
+            route_weights.T,
             residual,
             out_gate,
             attn_gain.reshape(1, columns),
             moe_gain.reshape(1, columns),
-            routes,
-            route_weights,
             w_gate,
             w_up,
             w_down,

time: 47.1 us -> 37.2 us (0.79)
  Pallas kernels: 41.2 us -> 35.4 us
  local copies, waits for them, and re-layouts: 5.69 us -> 1.57 us
    pallas_call x1, Pallas kernels: 41.2 us -> 35.4 us  [shards(): pl.pallas_call(lambda *refs: kernel(n_seq, n_exp, n_rep, *refs), name='la...]
    unnamed x4 -> x1, local copies, waits for them, and re-layouts: 5.69 us -> 1.57 us
where the time goes in v2:
time: 37.2 us; the launch traced here: 37 us
  Pallas kernels  35.4 us (95%)
  local copies, waits for them, and re-layouts  1.57 us (4%)
    pallas_call x1, Pallas kernels, shards(): pl.pallas_call(lambda *refs: kernel(n_seq, n_exp, n_rep, *refs), name='la...  35.4 us
    unnamed x1, local copies, waits for them, and re-layouts  1.57 us

profile of v2, /device:TPU:0, one launch (start us, length us, event | category | flops | bytes accessed | tf_op | source)
XLA Modules:
  0.0 37.0 jit_solution(9416178128178294948)
XLA Ops:
  0.0 35.4 %layer.1 = bf16[64,1024]{1,0:T(8,128)(2,1)} custom-call(bf16[64,1024]{1,0:T(8,128)(2,1)} %refs_0_.1, bf16[64,1024]{1,0:T(8,128)(2,1)} %refs_1_.1, f32[8,64]{1,0:T(8,128)} %bitcast.5, bf16[64,1024]{1,0:T(8,128)(2,1)} %refs_3_.1, s32[2,64]{1,0:T(2,128)} %bitcast.8, f32[2,64]{1,0:T(2,128)} %bitcast.9, bf16[64,1024]{1,0:T(8,128)(2,1)} %refs_6_.1, ...), custom_call_target="tpu_custom_call" | custom-call | tf_op jit(solution)/shard_map/layer/pallas_call | solution.py:470
  35.5 1.6 %copy.15 = bf16[64,1024]{1,0:T(8,128)(2,1)} copy(bf16[64,1024]{1,0:T(8,128)(2,1)} %layer.1) | data formatting | bytes 262144

commit v3 on v2

--- a/solution.py
+++ b/solution.py
@@ -71,7 +71,6 @@
     back,
     in_sem,
     w_sem,
-    up_sem,
     go_sem,
     chain_send,
     chain_recv,
@@ -190,13 +189,6 @@
             for p in range(PARTS):
                 hop(h, p).start()
 
-    def raise_hand():
-        pl.semaphore_signal(up_sem, inc=1, device_id={"seq": z - 1}, device_id_type=MESH)
-
-    @pl.when(z == last)
-    def _():
-        raise_hand()
-
     inputs[3].wait()
 
     for h in range(heads):
@@ -205,14 +197,6 @@
         gaps = cum[:, h : h + 1] - cum_t[h : h + 1, :]
         mixing = jnp.where(causal, scores * jnp.exp(jnp.where(causal, gaps, 0.0)), 0.0)
         att[:, cols] = jnp.dot(mixing.astype(BF16), v_ref[:, cols], preferred_element_type=F32)
-
-    @pl.when(z < last)
-    def _():
-        pl.semaphore_wait(up_sem, 1)
-
-        @pl.when(z > 0)
-        def _():
-            raise_hand()
 
     for load in inputs[4:]:
         load.wait()
@@ -311,7 +295,8 @@
         ).start()
 
     def deal_rows(e, to):
-        deal(e, to, pack.at[e], rows.at[r, here], disp_send, disp_recv)
+        used = pl.ds(0, CAP)
+        deal(e, to, pack.at[e, used], rows.at[r, here, used], disp_send, disp_recv)
 
     def earlier(send):
         def one(i):
@@ -343,7 +328,7 @@
         pl.semaphore_wait(go_sem, 1)
 
     later(deal_rows)
-    arrived = rows.at[r, pl.ds(0, plane - 1)]
+    arrived = rows.at[r, pl.ds(0, plane - 1), pl.ds(0, CAP)]
     pltpu.make_async_copy(arrived, arrived, disp_recv).wait()
     swap = pltpu.make_async_remote_copy(
         src_ref=rows.at[r],
@@ -407,18 +392,22 @@
     back[here_back] = fin[here_back]
 
     def hand_back(e, to):
-        deal(e, to, fin.at[e * n_seq + to], back.at[here_back], back_send, back_recv)
+        used = pl.ds(0, CAP)
+        source = fin.at[e * n_seq + to, used]
+        deal(e, to, source, back.at[here_back, used], back_send, back_recv)
 
     earlier(hand_back)
     later(hand_back)
     level(hand_back)
-    returned = back.at[pl.ds(0, plane - 1)]
+    returned = back.at[pl.ds(0, plane - 1), pl.ds(0, CAP)]
     pltpu.make_async_copy(returned, returned, back_recv).wait()
     coarse = combine.astype(BF16)
     fine = (combine - coarse.astype(F32)).astype(BF16)
     result = u_buf[...]
     for e in range(n_exp):
-        rows_e = jnp.sum(back[pl.ds(e * n_seq, n_seq)].astype(F32), axis=0).astype(BF16)
+        rows_e = jnp.sum(back[pl.ds(e * n_seq, n_seq)].astype(F32), axis=0)
+        slot = lax.broadcasted_iota(jnp.int32, rows_e.shape, 0)
+        rows_e = jnp.where(slot < CAP, rows_e, 0.0).astype(BF16)
         lanes = slice(e * SLOTS, (e + 1) * SLOTS)
         result += jnp.dot(coarse[:, lanes], rows_e, preferred_element_type=F32)
         result += jnp.dot(fine[:, lanes], rows_e, preferred_element_type=F32)
@@ -502,7 +491,6 @@
                 dma((10,)),
                 dma((3,)),
                 pltpu.SemaphoreType.REGULAR,
-                pltpu.SemaphoreType.REGULAR,
                 dma((heads, PARTS)),
                 dma((heads, PARTS)),
                 dma,

time: 37.2 us -> 35.8 us (0.962)
  Pallas kernels: 35.4 us -> 34.1 us
    pallas_call x1, Pallas kernels: 35.4 us -> 34.1 us  [shards(): pl.pallas_call(lambda *refs: kernel(n_seq, n_exp, n_rep, *refs), name='la...]
where the time goes in v3:
time: 35.8 us; the launch traced here: 35.6 us
  Pallas kernels  34.1 us (95%)
  local copies, waits for them, and re-layouts  1.57 us (4%)
    pallas_call x1, Pallas kernels, shards(): pl.pallas_call(lambda *refs: kernel(n_seq, n_exp, n_rep, *refs), name='la...  34.1 us
    unnamed x1, local copies, waits for them, and re-layouts  1.57 us

profile of v3, /device:TPU:0, one launch (start us, length us, event | category | flops | bytes accessed | tf_op | source)
XLA Modules:
  0.0 35.6 jit_solution(2315297453998371589)
XLA Ops:
  0.0 34.1 %layer.1 = bf16[64,1024]{1,0:T(8,128)(2,1)} custom-call(bf16[64,1024]{1,0:T(8,128)(2,1)} %refs_0_.1, bf16[64,1024]{1,0:T(8,128)(2,1)} %refs_1_.1, f32[8,64]{1,0:T(8,128)} %bitcast.5, bf16[64,1024]{1,0:T(8,128)(2,1)} %refs_3_.1, s32[2,64]{1,0:T(2,128)} %bitcast.8, f32[2,64]{1,0:T(2,128)} %bitcast.9, bf16[64,1024]{1,0:T(8,128)(2,1)} %refs_6_.1, ...), custom_call_target="tpu_custom_call" | custom-call | tf_op jit(solution)/shard_map/layer/pallas_call | solution.py:459
  34.1 1.6 %copy.15 = bf16[64,1024]{1,0:T(8,128)(2,1)} copy(bf16[64,1024]{1,0:T(8,128)(2,1)} %layer.1) | data formatting | bytes 262144
